TPU v7x, 32 devices: a whole 2x2x4 slice. The times are simulated.
32 devices in a mesh: section: 2 (over y), dp: 4 (over x, core), mp: 4 (over z).
Axes of the slice: x: 2, y: 2, z: 4, core: 2. Of those that a mesh axis runs over, the one named last changes fastest.
Arguments:
- patches: bfloat16 [4096, 1280], P(('section', 'dp')), may hold values from -6 to 6
- patch_counts: int32 [16], P(('section', 'dp')), may hold values from 64 to 256, as said below
- dest_rows: int32 [1024], P(('section', 'dp')), may hold values from 0 to 4095, as said below
- qkv_weight: bfloat16 [1280, 3, 1280], P(None, None, 'mp'), may hold values from -1 to 1
- out_weight: bfloat16 [1280, 1280], P('mp'), may hold values from -0.15625 to 0.15625
- attn_gain: bfloat16 [1280], replicated, may hold values from 0.25 to 1.75
- merge_gain: bfloat16 [1280], replicated, may hold values from 0.25 to 1.75
- fc1_weight: bfloat16 [5120, 5120], P('mp', ('section', 'dp')), may hold values from -0.078125 to 0.078125
- fc1_bias: bfloat16 [5120], P(('section', 'dp')), may hold values from -3 to 3
- fc2_weight: bfloat16 [5120, 8192], P(('section', 'dp'), 'mp'), may hold values from -0.078125 to 0.078125
- fc2_bias: bfloat16 [8192], P('mp'), may hold values from -3 to 3
- text_embeds: bfloat16 [4096, 8192], P(('section', 'dp'), 'mp'), may hold values from -6 to 6
- section_hidden: bfloat16 [4096, 8192], P(('section', 'dp'), 'mp'), may hold values from -80 to 80
- llm_gain: bfloat16 [8192], P('mp'), may hold values from 0.25 to 1.75
Outputs:
- sequence_embeds: bfloat16 [4096, 8192], P(('section', 'dp'), 'mp')
- layer_inputs: bfloat16 [4096, 8192], P(('section', 'dp'), 'mp')
Inputs may be any that keep to these rules, and one draw needn't show every extreme that they name: `patch_counts`: multiples of 4; a tile's patches fill the first slots of its block. `dest_rows`: all rows differ. Each group's merged slots form runs of 16 consecutive slots (aligned); a run goes to one sequence slice (row // 512, numbered in section-major order), different runs of a group to different slices. Rows of slots that are not live are never written.
All inputs are finite; a program needn't handle non-finite values.
Results may differ from a plain program's by a relative error of at most 0.0055.
Values may be sent and summed in bfloat16 or wider, within the bound.
A program may use at most 128 MiB of HBM per device.

v0:
```python
import jax
import jax.numpy as jnp
from jax import lax
from jax.sharding import PartitionSpec as P

HEAD_DIM = 80
HID = 8192
vit_eps = 1e-06
llm_eps = 1e-06


def from_behind(value, axis, steps):
    count = lax.axis_size(axis)
    first, last = (max(0, -steps), min(count, count - steps))
    return lax.ppermute(value, axis, [(source, source + steps) for source in range(first, last)])


def layer_norm(values, gain):
    centred = values.astype(jnp.float32)
    centred = centred - jnp.mean(centred, axis=-1, keepdims=True)
    variance = jnp.mean(centred * centred, axis=-1, keepdims=True)
    return centred * lax.rsqrt(variance + vit_eps) * gain.astype(jnp.float32)


def per_device(
    patches,
    patch_counts,
    dest_rows,
    qkv_weight,
    out_weight,
    attn_gain,
    merge_gain,
    fc1_weight,
    fc1_bias,
    fc2_weight,
    fc2_bias,
    text_embeds,
    section_hidden,
    llm_gain,
):
    width = patches.shape[1]
    tile_total = patch_counts.shape[0]
    block_rows = patches.shape[0] // tile_total
    merged_rows = patches.shape[0] // 4
    local_cols = qkv_weight.shape[2]
    local_heads = local_cols // HEAD_DIM
    feature_cols = text_embeds.shape[1]
    seq_rows = text_embeds.shape[0]
    section_count = lax.axis_size("section")
    group_count = section_count * lax.axis_size("dp")
    run_cap = max(2, merged_rows // group_count)
    run_total = merged_rows // run_cap
    normed_in = layer_norm(patches, attn_gain).astype(jnp.bfloat16)
    projections = jnp.dot(
        normed_in, qkv_weight.reshape(width, 3 * local_cols), preferred_element_type=jnp.float32
    ).astype(jnp.bfloat16)
    projections = projections.reshape(tile_total, block_rows, 3, local_heads, HEAD_DIM)
    query_part = projections[:, :, 0]
    key_part = projections[:, :, 1]
    value_part = projections[:, :, 2]
    scores = jnp.einsum(
        "tqhd,tkhd->thqk", query_part, key_part, preferred_element_type=jnp.float32
    ) * HEAD_DIM ** (-0.5)
    key_live = (
        jnp.arange(block_rows, dtype=jnp.int32)[None, None, None, :]
        < patch_counts[:, None, None, None]
    )
    scores = jnp.where(key_live, scores, -1e30)
    weights = jax.nn.softmax(scores, axis=-1).astype(jnp.bfloat16)
    attended = jnp.einsum(
        "thqk,tkhd->tqhd", weights, value_part, preferred_element_type=jnp.float32
    ).astype(jnp.bfloat16)
    attended = attended.reshape(patches.shape[0], local_cols)
    partial_proj = jnp.dot(attended, out_weight, preferred_element_type=jnp.float32)
    position = lax.axis_index("mp")
    own_patch = lax.dynamic_slice_in_dim(
        patches.reshape(merged_rows, 4, width), position, 1, 1
    ).reshape(merged_rows, width)
    own_proj = lax.psum_scatter(
        partial_proj.reshape(merged_rows, 4, width), "mp", scatter_dimension=1, tiled=True
    ).reshape(merged_rows, width)
    block_out = (own_patch.astype(jnp.float32) + own_proj).astype(jnp.bfloat16)
    merge_part = layer_norm(block_out, merge_gain).astype(jnp.bfloat16)
    first_full, second_full, bias_full = (
        lax.all_gather(fc1_weight, "section", axis=1, tiled=True),
        lax.all_gather(fc2_weight, "section", axis=0, tiled=True),
        lax.all_gather(fc1_bias, "section", axis=0, tiled=True),
    )
    first_partial = jnp.dot(
        lax.all_gather(merge_part, "dp", axis=0, tiled=True),
        first_full,
        preferred_element_type=jnp.float32,
    )
    first_total = lax.psum(first_partial, "mp")
    hidden = jax.nn.gelu(first_total + bias_full.astype(jnp.float32), approximate=False).astype(
        jnp.bfloat16
    )
    embed_total = lax.psum_scatter(
        jnp.dot(hidden, second_full, preferred_element_type=jnp.float32).astype(jnp.bfloat16),
        "dp",
        scatter_dimension=0,
        tiled=True,
    ).astype(jnp.float32)
    image_embeds = (embed_total + fc2_bias.astype(jnp.float32)).astype(jnp.bfloat16)
    slot_in_tile = jnp.arange(merged_rows, dtype=jnp.int32) % (block_rows // 4)
    tile_counts = jnp.repeat(patch_counts, block_rows // 4, total_repeat_length=merged_rows)
    live = slot_in_tile * 4 < tile_counts
    receiver = dest_rows // seq_rows
    run_target = receiver.reshape(run_total, run_cap)[:, 0]
    place = jnp.where(live, dest_rows % seq_rows, seq_rows)
    send_rows = (
        jnp.zeros((group_count, run_cap, feature_cols), jnp.bfloat16)
        .at[run_target]
        .set(image_embeds.reshape(run_total, run_cap, feature_cols))
    )
    send_place = (
        jnp.full((group_count, run_cap), seq_rows, jnp.int32)
        .at[run_target]
        .set(place.reshape(run_total, run_cap))
    )
    got_rows, got_place = (
        lax.all_to_all(send_rows, ("section", "dp"), split_axis=0, concat_axis=0, tiled=True),
        lax.all_to_all(send_place, ("section", "dp"), split_axis=0, concat_axis=0, tiled=True),
    )
    sequence_embeds = text_embeds.at[got_place.reshape(-1)].set(
        got_rows.reshape(-1, feature_cols), mode="drop"
    )
    incoming = from_behind(section_hidden, "section", 1)
    entering = jnp.where(lax.axis_index("section") == 0, sequence_embeds, incoming).astype(
        jnp.float32
    )
    row_total = lax.psum(jnp.sum(entering * entering, axis=1), "mp")
    layer_inputs = (
        entering * lax.rsqrt(row_total / HID + llm_eps)[:, None] * llm_gain.astype(jnp.float32)
    ).astype(jnp.bfloat16)
    return (sequence_embeds, layer_inputs)


def solution(mesh):
    in_specs = (
        P(("section", "dp"), None),
        P(("section", "dp")),
        P(("section", "dp")),
        P(None, None, "mp"),
        P("mp", None),
        P(),
        P(),
        P("mp", ("section", "dp")),
        P(("section", "dp")),
        P(("section", "dp"), "mp"),
        P("mp"),
        P(("section", "dp"), "mp"),
        P(("section", "dp"), "mp"),
        P("mp"),
    )
    out_specs = (P(("section", "dp"), "mp"), P(("section", "dp"), "mp"))
    return jax.shard_map(
        per_device, mesh=mesh, in_specs=in_specs, out_specs=out_specs, check_vma=False
    )
```

profile of v0, /device:TPU:0, one launch (start us, length us, event | category | flops | bytes accessed | tf_op | source)
XLA Modules:
  0.0 317.5 jit_solution(10290408837068384715)
XLA Ops:
  8.1 3.3 %copy.70 = bf16[512,2048]{1,0:T(8,128)(2,1)} copy(bf16[512,2048]{1,0:T(8,128)(2,1)} %param.27) | data formatting | bytes 4194304
  12.2 2.6 convolution_convert_fusion.1
  14.8 2.5 reshape.162
  17.3 1.6 fusion.107
  18.9 3.3 %fusion.109 = (f32[2,4,256]{2,1,0:T(4,128)S(1)}, f32[2,4,256,256]{2,3,1,0:T(8,128)}) fusion(pred[2,256]{1,0:T(4,128)(4,1)S(1)} %iota_compare_fusion, bf16[2,256,1,4,80]{1,0,4,3,2:T(2,128)(2,1)} %get-tuple-element.18, bf16[2,256,1,4,80]{1,0,4,3,2:T(2,128)(2,1)} %get-tuple-element.17), kind=kOutput, calls=%fused_computation.154 | convolution fusion | flops 85983488 | bytes 2761216 | tf_op jit(solution)/shard_map/sub | solution.py:69
  22.2 1.9 fusion.56
  24.9 3.5 %fusion.60 = f32[128,4,1280]{2,0,1:T(8,128)} fusion(bf16[320,1280]{1,0:T(8,128)(2,1)} %param.20, bf16[128,4,320]{2,1,0:T(4,128)(2,1)S(1)} %dot_general.23), kind=kOutput, calls=%fused_computation.82 | convolution fusion | flops 419430400 | bytes 3768320 | tf_op jit(solution)/shard_map/dot_general | solution.py:74
  29.1 3.5 %reshape.160 = bf16[128,4,1280]{2,1,0:T(4,128)(2,1)} reshape(bf16[512,1280]{1,0:T(8,128)(2,1)} %param.16) | data formatting | bytes 2621440 | tf_op jit(solution)/shard_map/reshape | solution.py:77
  32.6 2.0 constant_dynamic-slice_fusion
  34.6 49.0 %reduce-scatter.3.cloned.1.call-done = f32[128,1,1280]{2,0,1:T(8,128)} async-done(((f32[128,4,1280]{2,0,1:T(8,128)}), f32[128,1,1280]{2,0,1:T(8,128)}) %reduce-scatter.3.cloned.1.call-update) | async-done | bytes 655376 | tf_op jit(solution)/shard_map/reduce_scatter | solution.py:79
  83.6 1.2 convert_reduce_fusion.1
  85.1 1.0 fusion.67
  86.7 17.1 %all-gather.5.cloned.1.call-done = bf16[512,1280]{1,0:T(8,128)(2,1)} async-done(((bf16[128,1280]{1,0:T(8,128)(2,1)}), bf16[512,1280]{1,0:T(8,128)(2,1)}) %all-gather.5.cloned.1.call-update) | async-done | bytes 1310736 | tf_op jit(solution)/shard_map/all_gather | solution.py:90
  103.8 5.8 %fusion.110 = f32[512,1280]{1,0:T(8,128)} fusion(bf16[512,1280]{1,0:T(8,128)(2,1)} %all-gather.5.cloned.1.call-done, bf16[1280,1280]{1,0:T(8,128)(2,1)} %all-gather.7.cloned.1.call-done), kind=kOutput, calls=%fused_computation.155 | convolution fusion | flops 1677721600 | bytes 7208960 | tf_op jit(solution)/shard_map/dot_general | solution.py:89
  110.2 4.5 %all-gather = bf16[2,1,640]{2,1,0:T(2,128)(2,1)S(1)} all-gather(bf16[1,1,640]{2,1,0:T(2,128)(2,1)S(1)} %reshape.198), channel_id=1, replica_groups=mesh['section'=2,'dp'=4,'mp'=4] {'section'}, dimensions={0}, use_global_device_ids=true | all-gather | bytes 3840 | tf_op jit(solution)/shard_map/all_gather | solution.py:87
  114.8 58.8 %all-gather.9.cloned.1.call-done = bf16[1280,2048]{1,0:T(8,128)(2,1)} async-done(((bf16[640,2048]{1,0:T(8,128)(2,1)}), bf16[1280,2048]{1,0:T(8,128)(2,1)}) %all-gather.9.cloned.1.call-update) | async-done | bytes 5242896 | tf_op jit(solution)/shard_map/all_gather | solution.py:86
  173.6 40.2 %all-reduce.2.cloned.1.call-done = f32[512,1280]{1,0:T(8,128)} async-done(((f32[512,1280]{1,0:T(8,128)}), f32[512,1280]{1,0:T(8,128)}) %all-reduce.2.cloned.1.call-update) | async-done | bytes 2621456 | tf_op jit(solution)/shard_map/psum | solution.py:94
  213.8 12.1 %convolution_convert_fusion = bf16[512,2048]{1,0:T(8,128)(2,1)} fusion(bf16[1280,2048]{1,0:T(8,128)(2,1)} %all-gather.9.cloned.1.call-done, f32[512,1280]{1,0:T(8,128)} %all-reduce.2.cloned.1.call-done, f32[1280]{0:T(1024)S(1)} %reshape.200), kind=kOutput, calls=%fused_computation.14 | convolution fusion | flops 2728656896 | bytes 9966592 | tf_op jit(solution)/shard_map/dot_general | solution.py:99
  225.9 4.7 %collective-permute-start = (bf16[512,2048]{1,0:T(8,128)(2,1)}, bf16[512,2048]{1,0:T(8,128)(2,1)}, u32[]{:S(2)}, u32[]{:S(2)}) collective-permute-start(bf16[512,2048]{1,0:T(8,128)(2,1)} %param.28), channel_id=1, source_target_pairs={{0,16},{1,17},{2,18},{3,19},{4,20},{5,21},{6,22},{7,23},{8,24},{9,... | collective-permute-start | bytes 6291464 | tf_op jit(solution)/shard_map/ppermute | solution.py:15
  231.3 1.3 compare_select_fusion.2
  232.8 1.2 scatter_custom_fusion
  234.0 3.3 %all-to-all-start = ((s32[8,1,16]{2,1,0:T(1,128)}), s32[8,1,16]{2,1,0:T(1,128)S(1)}, u32[]{:S(2)}, u32[]{:S(2)}) async-start(s32[8,1,16]{2,1,0:T(1,128)} %bitcast.3), calls=%async_computation | async-start | bytes 8192 | tf_op jit(solution)/shard_map/all_to_all | solution.py:123
  237.3 19.0 %reduce-scatter.5.cloned.1.call-done = bf16[128,2048]{1,0:T(8,128)(2,1)} async-done(((bf16[512,2048]{1,0:T(8,128)(2,1)}), bf16[128,2048]{1,0:T(8,128)(2,1)}) %reduce-scatter.5.cloned.1.call-update) | async-done | bytes 524304 | tf_op jit(solution)/shard_map/reduce_scatter | solution.py:98
  256.3 1.1 add_convert_fusion
  258.3 2.4 scatter_fusion
  260.7 13.7 %all-to-all-done = s32[8,1,16]{2,1,0:T(1,128)S(1)} async-done(((s32[8,1,16]{2,1,0:T(1,128)}), s32[8,1,16]{2,1,0:T(1,128)S(1)}, u32[]{:S(2)}, u32[]{:S(2)}) %all-to-all-start) | async-done | bytes 544 | tf_op jit(solution)/shard_map/all_to_all | solution.py:123
  274.4 4.7 %all-to-all-start.1 = ((bf16[8,16,2048]{2,1,0:T(8,128)(2,1)}), bf16[8,16,2048]{2,1,0:T(8,128)(2,1)S(1)}, u32[]{:S(2)}, u32[]{:S(2)}) async-start(bf16[8,16,2048]{2,1,0:T(8,128)(2,1)} %scatter_fusion), calls=%async_computation.3 | async-start | bytes 1048576 | tf_op jit(solution)/shard_map/all_to_all | solution.py:122
  280.3 8.5 %all-to-all-done.1 = bf16[8,16,2048]{2,1,0:T(8,128)(2,1)S(1)} async-done(((bf16[8,16,2048]{2,1,0:T(8,128)(2,1)}), bf16[8,16,2048]{2,1,0:T(8,128)(2,1)S(1)}, u32[]{:S(2)}, u32[]{:S(2)}) %all-to-all-start.1) | async-done | bytes 524320 | tf_op jit(solution)/shard_map/all_to_all | solution.py:122
  288.8 4.6 %scatter_fusion.1 = bf16[512,2048]{1,0:T(8,128)(2,1)} fusion(bf16[512,2048]{1,0:T(8,128)(2,1)} %copy.70, s32[128]{0:T(128)S(1)} %fusion.74, bf16[128,2048]{1,0:T(8,128)(2,1)S(1)} %bitcast.61), kind=kCustom, calls=%fused_computation.2 | custom fusion | bytes 1573376 | tf_op jit(solution)/shard_map/scatter | solution.py:125
  293.4 2.3 fusion.1
  295.7 10.0 %psum.15 = f32[512]{0:T(512)S(1)} all-reduce(f32[512]{0:T(512)S(1)} %fusion.1), channel_id=1, replica_groups=mesh['section'=2,'dp'=4,'mp'=4] {'mp'}, use_global_device_ids=true, to_apply=%region_13.14 | all-reduce | flops 512 | bytes 4096 | tf_op jit(solution)/shard_map/psum | solution.py:132
  305.8 4.1 %fusion.3 = bf16[512,2048]{1,0:T(8,128)(2,1)} fusion(f32[2048]{0:T(1024)S(1)} %convert_element_type.88, f32[512]{0:T(512)S(1)} %add_rsqrt_fusion, bf16[512,2048]{1,0:T(8,128)(2,1)} %scatter_fusion.1, bf16[512,2048]{1,0:T(8,128)(2,1)} %collective-permute-done, pred[]{:T(512)S(6)} %eq.6), kind=kLoop, calls=%fused_computation.8 | loop fusion | flops 5242880 | bytes 6301697 | tf_op jit(solution)/shard_map/convert_element_type | solution.py:135
  (63 shorter events, 6.9 us)
Async XLA Ops:
  8.0 4.2 %copy-start = (bf16[1280,3,320]{0,2,1:T(8,128)(2,1)S(1)}, bf16[1280,3,320]{0,2,1:T(8,128)(2,1)}, u32[]{:S(2)}) copy-start(bf16[1280,3,320]{0,2,1:T(8,128)(2,1)} %param.19) | copy-start | bytes 7372804
  8.0 4.1 %copy-start.3 = (bf16[1280]{0:T(1024)(128)(2,1)S(1)}, bf16[1280]{0:T(1024)(128)(2,1)}, u32[]{:S(2)}) copy-start(bf16[1280]{0:T(1024)(128)(2,1)} %param.21) | copy-start | bytes 7684
  8.0 75.6 %reduce-scatter.3.cloned.1.call-start = ((), (), s32[]{:S(2)}) async-start(), calls=%async_computation.4 | async-start | bytes 3276800 | tf_op jit(solution)/shard_map/reduce_scatter | solution.py:79
  8.1 3.3 %copy-start.1 = (bf16[512,1280]{1,0:T(8,128)(2,1)S(1)}, bf16[512,1280]{1,0:T(8,128)(2,1)}, u32[]{:S(2)}) copy-start(bf16[512,1280]{1,0:T(8,128)(2,1)} %param.16) | copy-start | bytes 3932164
  14.8 4.1 %copy-start.8 = (s32[2]{0:T(128)S(1)}, s32[2]{0:T(128)}, u32[]{:S(2)}) copy-start(s32[2]{0:T(128)} %param.17) | copy-start | bytes 28
  18.9 3.4 %copy-start.2 = (bf16[2,256,1,4,80]{1,0,4,3,2:T(2,128)(2,1)S(1)}, bf16[2,256,1,4,80]{1,0,4,3,2:T(2,128)(2,1)}, u32[]{:S(2)}) copy-start(bf16[2,256,1,4,80]{1,0,4,3,2:T(2,128)(2,1)} %get-tuple-element.16) | copy-start | bytes 983044
  28.5 4.1 %copy-start.4 = (bf16[1280]{0:T(1024)(128)(2,1)S(1)}, bf16[1280]{0:T(1024)(128)(2,1)}, u32[]{:S(2)}) copy-start(bf16[1280]{0:T(1024)(128)(2,1)} %param.22) | copy-start | bytes 7684
  28.5 58.3 %all-gather.7.cloned.1.call-start = ((), (), s32[]{:S(2)}) async-start(), calls=%async_computation.6 | async-start | bytes 4915200 | tf_op jit(solution)/shard_map/all_gather | solution.py:85
  29.1 74.7 %all-gather.5.cloned.1.call-start = ((), (), s32[]{:S(2)}) async-start(), calls=%async_computation.5 | async-start | bytes 1638400 | tf_op jit(solution)/shard_map/all_gather | solution.py:90
  86.1 87.6 %all-gather.9.cloned.1.call-start = ((), (), s32[]{:S(2)}) async-start(), calls=%async_computation.8 | async-start | bytes 7864320 | tf_op jit(solution)/shard_map/all_gather | solution.py:86
  86.6 127.2 %all-reduce.2.cloned.1.call-start = ((), (), s32[]{:S(2)}) async-start(), calls=%async_computation.7 | async-start | bytes 5242880 | tf_op jit(solution)/shard_map/psum | solution.py:94
  109.5 0.7 copy-start.7
  109.6 146.7 %reduce-scatter.5.cloned.1.call-start = ((), (), s32[]{:S(2)}) async-start(), calls=%async_computation.9 | async-start | bytes 2621440 | tf_op jit(solution)/shard_map/reduce_scatter | solution.py:98
  114.8 116.5 %copy-start.9 = (s32[128]{0:T(128)S(1)}, s32[128]{0:T(128)}, u32[]{:S(2)}) copy-start(s32[128]{0:T(128)} %param.18) | copy-start | bytes 1540
  114.8 116.5 %copy-start.10 = (pred[128]{0:T(512)(128)(4,1)S(1)}, pred[128]{0:T(512)(128)(4,1)}, u32[]{:S(2)}) copy-start(pred[128]{0:T(512)(128)(4,1)} %constant.224) | copy-start | bytes 388
  114.8 122.4 %copy-start.5 = (bf16[2048]{0:T(1024)(128)(2,1)S(1)}, bf16[2048]{0:T(1024)(128)(2,1)}, u32[]{:S(2)}) copy-start(bf16[2048]{0:T(1024)(128)(2,1)} %param.26) | copy-start | bytes 12292
  225.9 53.1 %copy-start.6 = (bf16[2048]{0:T(1024)(128)(2,1)S(1)}, bf16[2048]{0:T(1024)(128)(2,1)}, u32[]{:S(2)}) copy-start(bf16[2048]{0:T(1024)(128)(2,1)} %param.29) | copy-start | bytes 12292
  225.9 67.4 %collective-permute-start = (bf16[512,2048]{1,0:T(8,128)(2,1)}, bf16[512,2048]{1,0:T(8,128)(2,1)}, u32[]{:S(2)}, u32[]{:S(2)}) collective-permute-start(bf16[512,2048]{1,0:T(8,128)(2,1)} %param.28), channel_id=1, source_target_pairs={{0,16},{1,17},{2,18},{3,19},{4,20},{5,21},{6,22},{7,23},{8,24},{9,... | collective-permute-start | bytes 6291464 | tf_op jit(solution)/shard_map/ppermute | solution.py:15
  234.0 40.4 %all-to-all-start = ((s32[8,1,16]{2,1,0:T(1,128)}), s32[8,1,16]{2,1,0:T(1,128)S(1)}, u32[]{:S(2)}, u32[]{:S(2)}) async-start(s32[8,1,16]{2,1,0:T(1,128)} %bitcast.3), calls=%async_computation | async-start | bytes 8192 | tf_op jit(solution)/shard_map/all_to_all | solution.py:123
  274.4 14.4 %all-to-all-start.1 = ((bf16[8,16,2048]{2,1,0:T(8,128)(2,1)}), bf16[8,16,2048]{2,1,0:T(8,128)(2,1)S(1)}, u32[]{:S(2)}, u32[]{:S(2)}) async-start(bf16[8,16,2048]{2,1,0:T(8,128)(2,1)} %scatter_fusion), calls=%async_computation.3 | async-start | bytes 1048576 | tf_op jit(solution)/shard_map/all_to_all | solution.py:122
Sparse Core Ops, SparseCore 0:
  28.6 54.9 reduce-scatter.2
  109.7 104.0 all-reduce.1
Sparse Core Ops, SparseCore 1:
  30.5 48.9 all-gather.6
  86.2 17.6 all-gather.4
  105.2 68.4 all-gather.8
  226.0 30.2 reduce-scatter.4
where the time goes:
time: 318 us; the launch traced here: 317 us
  waiting for transfers between devices  207 us (65%)
  matrix products  29.1 us (9%)
  local copies, waits for them, and re-layouts  24.8 us (8%)
  between operations  15.9 us (5%)
  blocking collectives  14.6 us (5%)
  starting transfers between devices  12.9 us (4%)
  other arithmetic  12.9 us (4%)
    all_gather x1, waiting for transfers between devices, per_device(): lax.all_gather(fc2_weight, 'section', axis=0, tiled=True)  58.8 us
    reduce_scatter x1, waiting for transfers between devices, per_device(): lax.psum_scatter(partial_proj.reshape(merged_rows, 4, width), 'mp', scatt...  49 us
    psum x1, waiting for transfers between devices, per_device(): first_total = lax.psum(first_partial, 'mp')  40.2 us
    reduce_scatter x1, waiting for transfers between devices, per_device(): lax.psum_scatter(jnp.dot(hidden, second_full, preferred_element_type=jnp....  19 us
    all_gather x1, waiting for transfers between devices, per_device(): lax.all_gather(merge_part, 'dp', axis=0, tiled=True)  17.1 us
    all_to_all x1, waiting for transfers between devices, per_device(): lax.all_to_all(send_place, ('section', 'dp'), split_axis=0, concat_axis=0...  13.7 us
    dot_general x1, matrix products, per_device(): jnp.dot(hidden, second_full, preferred_element_type=jnp.float32)  12.1 us
    psum x1, blocking collectives, per_device(): row_total = lax.psum(jnp.sum(entering * entering, axis=1), 'mp')  10 us
  transfers between devices with their start and end apart: 9, of which 7 were waited for; matrix products, arithmetic and copies ran while one was open for 9% of the time, Pallas kernels for 0%

commit v1 on v0

--- a/solution.py
+++ b/solution.py
@@ -7,6 +7,11 @@
 HID = 8192
 vit_eps = 1e-06
 llm_eps = 1e-06
+
+
+def summed_here(x, mesh_axis):
+    parts = lax.all_gather(x, mesh_axis)
+    return jnp.sum(parts, axis=0)
 
 
 def from_behind(value, axis, steps):
@@ -91,7 +96,7 @@
         first_full,
         preferred_element_type=jnp.float32,
     )
-    first_total = lax.psum(first_partial, "mp")
+    first_total = summed_here(first_partial, "mp")
     hidden = jax.nn.gelu(first_total + bias_full.astype(jnp.float32), approximate=False).astype(
         jnp.bfloat16
     )

time: 318 us -> 467 us (1.47)
  waiting for transfers between devices: 207 us -> 350 us
  other arithmetic: 12.9 us -> 19.4 us
    all_gather x0 -> x1, waiting for transfers between devices: none -> 179 us  [summed_here(): parts = lax.all_gather(x, mesh_axis)]
    psum x1 -> x0, waiting for transfers between devices: 40.2 us -> none  [per_device(): first_total = lax.psum(first_partial, 'mp')]
    reduce_sum x0 -> x1, other arithmetic: none -> 6.43 us  [summed_here(): return jnp.sum(parts, axis=0)]
  transfers between devices with their start and end apart: 9 -> 9, of which waited for: 7 -> 7; matrix products, arithmetic and copies ran while one was open for 9% -> 6% of each run, Pallas kernels for 0% -> 0%
where the time goes in v1:
time: 467 us; the launch traced here: 466 us
  waiting for transfers between devices  350 us (75%)
  matrix products  29.1 us (6%)
  local copies, waits for them, and re-layouts  24.2 us (5%)
  other arithmetic  19.4 us (4%)
  blocking collectives  16.2 us (3%)
  between operations  15.6 us (3%)
  starting transfers between devices  11.8 us (3%)
    all_gather x1, waiting for transfers between devices, summed_here(): parts = lax.all_gather(x, mesh_axis)  179 us
    all_gather x1, waiting for transfers between devices, per_device(): lax.all_gather(fc2_weight, 'section', axis=0, tiled=True)  61.9 us
    reduce_scatter x1, waiting for transfers between devices, per_device(): lax.psum_scatter(partial_proj.reshape(merged_rows, 4, width), 'mp', scatt...  49 us
    reduce_scatter x1, waiting for transfers between devices, per_device(): lax.psum_scatter(jnp.dot(hidden, second_full, preferred_element_type=jnp....  21.1 us
    all_gather x1, waiting for transfers between devices, per_device(): lax.all_gather(merge_part, 'dp', axis=0, tiled=True)  17.6 us
    dot_general x1, matrix products, per_device(): jnp.dot(hidden, second_full, preferred_element_type=jnp.float32)  12.1 us
    all_to_all x1, waiting for transfers between devices, per_device(): lax.all_to_all(send_place, ('section', 'dp'), split_axis=0, concat_axis=0...  11.8 us
    psum x1, blocking collectives, per_device(): row_total = lax.psum(jnp.sum(entering * entering, axis=1), 'mp')  11.7 us
  transfers between devices with their start and end apart: 9, of which 7 were waited for; matrix products, arithmetic and copies ran while one was open for 6% of the time, Pallas kernels for 0%

profile of v1, /device:TPU:0, one launch (start us, length us, event | category | flops | bytes accessed | tf_op | source)
XLA Modules:
  0.0 466.0 jit_solution(1850547975907895341)
XLA Ops:
  8.1 3.3 copy.69
  12.2 2.6 convolution_convert_fusion.1
  14.8 2.5 reshape.162
  17.3 1.6 fusion.107
  18.9 3.3 fusion.109
  22.2 1.9 fusion.56
  24.9 3.5 fusion.60
  29.1 3.5 reshape.160
  32.6 2.0 constant_dynamic-slice_fusion
  34.6 49.0 %reduce-scatter.3.cloned.1.call-done = f32[128,1,1280]{2,0,1:T(8,128)} async-done(((f32[128,4,1280]{2,0,1:T(8,128)}), f32[128,1,1280]{2,0,1:T(8,128)}) %reduce-scatter.3.cloned.1.call-update) | async-done | bytes 655376 | tf_op jit(solution)/shard_map/reduce_scatter | solution.py:84
  83.6 1.2 convert_reduce_fusion.1
  86.2 17.6 %all-gather.7.cloned.1.call-done = bf16[512,1280]{1,0:T(8,128)(2,1)} async-done(((bf16[128,1280]{1,0:T(8,128)(2,1)}), bf16[512,1280]{1,0:T(8,128)(2,1)}) %all-gather.7.cloned.1.call-update) | async-done | bytes 1310736 | tf_op jit(solution)/shard_map/all_gather | solution.py:95
  103.8 5.7 %fusion.110 = f32[512,1280]{1,0:T(8,128)} fusion(bf16[512,1280]{1,0:T(8,128)(2,1)} %all-gather.7.cloned.1.call-done, bf16[1280,1280]{1,0:T(8,128)(2,1)} %all-gather.9.cloned.1.call-done), kind=kOutput, calls=%fused_computation.155 | convolution fusion | flops 1677721600 | bytes 7208960 | tf_op jit(solution)/shard_map/dot_general | solution.py:94
  110.3 4.5 all-gather.1
  114.9 178.7 %all-gather.13.cloned.1.call-done = f32[2048,1280]{1,0:T(8,128)} async-done(((f32[512,1280]{1,0:T(8,128)}), f32[2048,1280]{1,0:T(8,128)}) %all-gather.13.cloned.1.call-update) | async-done | bytes 10485776 | tf_op jit(solution)/shard_map/all_gather | solution.py:13
  293.6 6.4 %reduce_sum.68 = f32[512,1280]{1,0:T(8,128)} reduce(f32[4,512,1280]{2,1,0:T(8,128)} %bitcast.62, f32[]{:T(128)} %constant.182.clone.1), dimensions={0}, to_apply=%region_8.9 | reduce | flops 1966080 | bytes 13107204 | tf_op jit(solution)/shard_map/reduce_sum | solution.py:14
  300.0 61.9 %all-gather.11.cloned.1.call-done = bf16[1280,2048]{1,0:T(8,128)(2,1)} async-done(((bf16[640,2048]{1,0:T(8,128)(2,1)}), bf16[1280,2048]{1,0:T(8,128)(2,1)}) %all-gather.11.cloned.1.call-update) | async-done | bytes 5242896 | tf_op jit(solution)/shard_map/all_gather | solution.py:91
  361.9 12.1 %convolution_convert_fusion = bf16[512,2048]{1,0:T(8,128)(2,1)} fusion(bf16[1280,2048]{1,0:T(8,128)(2,1)} %all-gather.11.cloned.1.call-done, f32[512,1280]{1,0:T(8,128)} %reduce_sum.68, f32[1280]{0:T(1024)S(1)} %reshape.201), kind=kOutput, calls=%fused_computation.14 | convolution fusion | flops 2728656896 | bytes 9966592 | tf_op jit(solution)/shard_map/dot_general | solution.py:104
  374.0 3.6 collective-permute-start
  378.2 1.3 compare_select_fusion.2
  379.8 1.2 scatter_custom_fusion
  380.9 3.3 all-to-all-start
  384.2 21.1 %reduce-scatter.5.cloned.1.call-done = bf16[128,2048]{1,0:T(8,128)(2,1)} async-done(((bf16[512,2048]{1,0:T(8,128)(2,1)}), bf16[128,2048]{1,0:T(8,128)(2,1)}) %reduce-scatter.5.cloned.1.call-update) | async-done | bytes 524304 | tf_op jit(solution)/shard_map/reduce_scatter | solution.py:103
  405.3 1.1 add_convert_fusion
  407.3 2.4 scatter_fusion
  409.7 11.8 %all-to-all-done = s32[8,1,16]{2,1,0:T(1,128)S(1)} async-done(((s32[8,1,16]{2,1,0:T(1,128)}), s32[8,1,16]{2,1,0:T(1,128)S(1)}, u32[]{:S(2)}, u32[]{:S(2)}) %all-to-all-start) | async-done | bytes 544 | tf_op jit(solution)/shard_map/all_to_all | solution.py:128
  421.5 4.7 %all-to-all-start.1 = ((bf16[8,16,2048]{2,1,0:T(8,128)(2,1)}), bf16[8,16,2048]{2,1,0:T(8,128)(2,1)S(1)}, u32[]{:S(2)}, u32[]{:S(2)}) async-start(bf16[8,16,2048]{2,1,0:T(8,128)(2,1)} %scatter_fusion), calls=%async_computation.3 | async-start | bytes 1048576 | tf_op jit(solution)/shard_map/all_to_all | solution.py:127
  427.5 8.5 %all-to-all-done.1 = bf16[8,16,2048]{2,1,0:T(8,128)(2,1)S(1)} async-done(((bf16[8,16,2048]{2,1,0:T(8,128)(2,1)}), bf16[8,16,2048]{2,1,0:T(8,128)(2,1)S(1)}, u32[]{:S(2)}, u32[]{:S(2)}) %all-to-all-start.1) | async-done | bytes 524320 | tf_op jit(solution)/shard_map/all_to_all | solution.py:127
  435.9 4.6 scatter_fusion.1
  440.5 2.3 fusion.1
  442.9 11.7 %psum.7 = f32[512]{0:T(512)S(1)} all-reduce(f32[512]{0:T(512)S(1)} %fusion.1), channel_id=1, replica_groups=mesh['section'=2,'dp'=4,'mp'=4] {'mp'}, use_global_device_ids=true, to_apply=%region_13.14 | all-reduce | flops 512 | bytes 4096 | tf_op jit(solution)/shard_map/psum | solution.py:137
  454.6 4.1 fusion.3
  (64 shorter events, 7.4 us)
Async XLA Ops:
  8.0 4.2 copy-start
  8.0 4.1 copy-start.3
  8.0 75.6 %reduce-scatter.3.cloned.1.call-start = ((), (), s32[]{:S(2)}) async-start(), calls=%async_computation.4 | async-start | bytes 3276800 | tf_op jit(solution)/shard_map/reduce_scatter | solution.py:84
  8.1 3.3 copy-start.1
  14.8 4.1 copy-start.8
  18.9 3.4 copy-start.2
  28.5 4.1 copy-start.4
  28.5 57.7 %all-gather.9.cloned.1.call-start = ((), (), s32[]{:S(2)}) async-start(), calls=%async_computation.6 | async-start | bytes 4915200 | tf_op jit(solution)/shard_map/all_gather | solution.py:90
  29.1 74.7 %all-gather.7.cloned.1.call-start = ((), (), s32[]{:S(2)}) async-start(), calls=%async_computation.5 | async-start | bytes 1638400 | tf_op jit(solution)/shard_map/all_gather | solution.py:95
  86.1 207.5 %all-gather.13.cloned.1.call-start = ((), (), s32[]{:S(2)}) async-start(), calls=%async_computation.9 | async-start | bytes 13107200 | tf_op jit(solution)/shard_map/all_gather | solution.py:13
  109.5 0.8 copy-start.7
  109.5 252.4 %all-gather.11.cloned.1.call-start = ((), (), s32[]{:S(2)}) async-start(), calls=%async_computation.7 | async-start | bytes 7864320 | tf_op jit(solution)/shard_map/all_gather | solution.py:91
  110.2 295.1 %reduce-scatter.5.cloned.1.call-start = ((), (), s32[]{:S(2)}) async-start(), calls=%async_computation.8 | async-start | bytes 2621440 | tf_op jit(solution)/shard_map/reduce_scatter | solution.py:103
  300.0 78.2 %copy-start.9 = (s32[128]{0:T(128)S(1)}, s32[128]{0:T(128)}, u32[]{:S(2)}) copy-start(s32[128]{0:T(128)} %param.18) | copy-start | bytes 1540
  300.0 78.2 %copy-start.10 = (pred[128]{0:T(512)(128)(4,1)S(1)}, pred[128]{0:T(512)(128)(4,1)}, u32[]{:S(2)}) copy-start(pred[128]{0:T(512)(128)(4,1)} %constant.224) | copy-start | bytes 388
  300.0 84.2 %copy-start.5 = (bf16[2048]{0:T(1024)(128)(2,1)S(1)}, bf16[2048]{0:T(1024)(128)(2,1)}, u32[]{:S(2)}) copy-start(bf16[2048]{0:T(1024)(128)(2,1)} %param.26) | copy-start | bytes 12292
  374.0 52.2 %copy-start.6 = (bf16[2048]{0:T(1024)(128)(2,1)S(1)}, bf16[2048]{0:T(1024)(128)(2,1)}, u32[]{:S(2)}) copy-start(bf16[2048]{0:T(1024)(128)(2,1)} %param.29) | copy-start | bytes 12292
  374.0 66.5 %collective-permute-start = (bf16[512,2048]{1,0:T(8,128)(2,1)}, bf16[512,2048]{1,0:T(8,128)(2,1)}, u32[]{:S(2)}, u32[]{:S(2)}) collective-permute-start(bf16[512,2048]{1,0:T(8,128)(2,1)} %param.28), channel_id=1, source_target_pairs={{0,16},{1,17},{2,18},{3,19},{4,20},{5,21},{6,22},{7,23},{8,24},{9,... | collective-permute-start | bytes 6291464 | tf_op jit(solution)/shard_map/ppermute | solution.py:20
  380.9 40.6 %all-to-all-start = ((s32[8,1,16]{2,1,0:T(1,128)}), s32[8,1,16]{2,1,0:T(1,128)S(1)}, u32[]{:S(2)}, u32[]{:S(2)}) async-start(s32[8,1,16]{2,1,0:T(1,128)} %bitcast.3), calls=%async_computation | async-start | bytes 8192 | tf_op jit(solution)/shard_map/all_to_all | solution.py:128
  421.5 14.4 %all-to-all-start.1 = ((bf16[8,16,2048]{2,1,0:T(8,128)(2,1)}), bf16[8,16,2048]{2,1,0:T(8,128)(2,1)S(1)}, u32[]{:S(2)}, u32[]{:S(2)}) async-start(bf16[8,16,2048]{2,1,0:T(8,128)(2,1)} %scatter_fusion), calls=%async_computation.3 | async-start | bytes 1048576 | tf_op jit(solution)/shard_map/all_to_all | solution.py:127
Sparse Core Ops, SparseCore 0:
  28.6 54.9 reduce-scatter.2
  109.6 183.8 all-gather.12
  295.1 66.7 all-gather.10
Sparse Core Ops, SparseCore 1:
  30.5 48.9 all-gather.8
  86.2 17.6 all-gather.6
  374.1 31.2 reduce-scatter.4
